TPU v7x, 32 devices: a whole 2x2x4 slice. The times are simulated.
32 devices in a mesh: grp: 4 (over z), dev: 8 (over y, x, core).
Axes of the slice: x: 2, y: 2, z: 4, core: 2. Of those that a mesh axis runs over, the one named last changes fastest.
Arguments:
- matrix_tiles: bfloat16 [640, 128, 1024], P(('grp', 'dev')), may hold values from -0.125 to 0.125
- tile_column: int32 [640], P(('grp', 'dev')), may hold values from 0 to 255
- block_counts: int32 [256], P(('grp', 'dev')), may hold values from 1 to 4, as said below
- destination: int32 [256], P(('grp', 'dev')), may hold values from 0 to 7, as said below
- row_bounds: bfloat16 [32768], P(('grp', 'dev')), may hold values from -6 to 6
- dual_start: bfloat16 [32768], P(('grp', 'dev')), may hold values from 0 to 1
- primal_start: float32 [262144], replicated, may hold values from 0 to 0.5
- cost_vector: float32 [262144], replicated, may hold values from -6 to 6
- upper_bound: float32 [262144], replicated, may hold values from 0.5 to 2
Outputs:
- primal_final: float32 [262144], replicated
- dual_final: float32 [32768], P(('grp', 'dev'))
- weight_final: float32 [1], replicated
Inputs may be any that keep to these rules, and one draw needn't show every extreme that they name: `block_counts`: each device's 8 row blocks have 1 to 4 tiles each and 20 at most together; some device has exactly 20 in every draw. `destination`: on every device the 8 entries are each of 0 to 7 once.
All inputs are finite; a program needn't handle non-finite values.
Results may differ from a plain program's by a relative error of at most 0.0015.
Values may be sent and summed in bfloat16 or wider, within the bound.
A program may use at most 128 MiB of HBM per device.

v0:
```python
import jax
import jax.numpy as jnp
from jax import lax
from jax.sharding import PartitionSpec as P

NCB = 256
ITERS = 3


step_scale = 0.3


def row_products(tile_store, vector_bf, blocks):
    tile_set, tile_cols, owners, live_flags = tile_store
    vector_table = vector_bf.reshape(-1, tile_set.shape[2])
    column_hot = (
        tile_cols[:, None] == jnp.arange(vector_table.shape[0], dtype=jnp.int32)[None, :]
    ).astype(jnp.bfloat16)
    picked = jnp.dot(column_hot, vector_table, preferred_element_type=jnp.float32).astype(
        jnp.bfloat16
    )
    product = jnp.einsum("src,sc->sr", tile_set, picked, preferred_element_type=jnp.float32)
    product = jnp.where(live_flags[:, None], product, 0.0)
    owner_hot = (jnp.arange(blocks, dtype=jnp.int32)[:, None] == owners[None, :]).astype(
        jnp.float32
    )
    return jnp.dot(owner_hot, product, precision=lax.Precision.HIGHEST)


def column_products(tile_store, rows_bf):
    tile_set, tile_cols, owners, live_flags = tile_store
    blocks = rows_bf.shape[0]
    owner_hot = (owners[:, None] == jnp.arange(blocks, dtype=jnp.int32)[None, :]).astype(
        jnp.bfloat16
    )
    picked_rows = jnp.dot(owner_hot, rows_bf, preferred_element_type=jnp.float32).astype(
        jnp.bfloat16
    )
    product = jnp.einsum("src,sr->sc", tile_set, picked_rows, preferred_element_type=jnp.float32)
    product = jnp.where(live_flags[:, None], product, 0.0)
    column_hot = (jnp.arange(NCB, dtype=jnp.int32)[:, None] == tile_cols[None, :]).astype(
        jnp.float32
    )
    return jnp.dot(column_hot, product, precision=lax.Precision.HIGHEST).reshape(-1)


def per_device(
    matrix_tiles,
    tile_column,
    block_counts,
    destination,
    row_bounds,
    dual_start,
    primal_start,
    cost_vector,
    upper_bound,
):
    blocks = block_counts.shape[0]
    rows_per = matrix_tiles.shape[1]
    slot_count = matrix_tiles.shape[0]
    starts = jnp.cumsum(block_counts) - block_counts
    slot_ids = jnp.arange(slot_count, dtype=jnp.int32)
    owners = jnp.sum((starts[None, 1:] <= slot_ids[:, None]).astype(jnp.int32), axis=1)
    bounds_here = row_bounds.reshape(blocks, rows_per)
    dual_here = dual_start.reshape(blocks, rows_per)
    peer_ids = jnp.arange(blocks, dtype=jnp.int32)
    inverse = jnp.sum(
        jnp.where(destination[None, :] == peer_ids[:, None], peer_ids[None, :], 0), axis=1
    )
    tile_store = (matrix_tiles, tile_column, owners, slot_ids < jnp.sum(block_counts))
    bounds = bounds_here.astype(jnp.float32)
    dual_state = dual_here.astype(jnp.float32)
    primal = primal_start
    weight = jnp.ones((), jnp.float32)
    row_image = row_products(tile_store, primal.astype(jnp.bfloat16), blocks)
    for iteration in range(ITERS):
        step_primal = step_scale / weight
        step_dual = step_scale * weight
        partial_value = column_products(tile_store, dual_state.astype(jnp.bfloat16))
        gradient = lax.psum(partial_value, ("grp", "dev"))
        primal_next = jnp.clip(primal - step_primal * (cost_vector - gradient), 0.0, upper_bound)
        change = jnp.sum((primal_next - primal) ** 2)
        next_image = row_products(tile_store, primal_next.astype(jnp.bfloat16), blocks)
        dual_state = jnp.maximum(
            dual_state + step_dual * (bounds - (2.0 * next_image - row_image)), 0.0
        )
        violation_part = jnp.sum(jnp.maximum(bounds - next_image, 0.0) ** 2)
        violation = lax.psum(violation_part, ("grp", "dev"))
        weight = jnp.sqrt(weight * jnp.sqrt((violation + 1e-06) / (change + 1e-06)))
        primal = primal_next
        row_image = next_image
    dual_final = lax.all_to_all(
        dual_state[inverse], "dev", split_axis=0, concat_axis=0, tiled=True
    ).reshape(-1)
    return (primal, dual_final, jnp.reshape(weight, (1,)))


def solution(mesh):
    in_specs = (
        P(("grp", "dev"), None, None),
        P(("grp", "dev")),
        P(("grp", "dev")),
        P(("grp", "dev")),
        P(("grp", "dev")),
        P(("grp", "dev")),
        P(),
        P(),
        P(),
    )
    out_specs = (P(), P(("grp", "dev")), P())
    return jax.shard_map(
        per_device, mesh=mesh, in_specs=in_specs, out_specs=out_specs, check_vma=False
    )
```

profile of v0, /device:TPU:0, one launch (start us, length us, event | category | flops | bytes accessed | tf_op | source)
XLA Modules:
  0.0 506.8 jit_solution(13658657499883403431)
XLA Ops:
  7.2 1.0 reduce-window.9
  8.2 1.3 fusion.92
  9.7 0.6 iota_compare_fusion.20
  10.3 0.9 fusion.4
  11.2 3.3 fusion.46
  14.5 0.6 convolution_bitcast_fusion.2
  15.1 1.2 copy.28
  16.3 133.6 %all-reduce.4.cloned.1.call-done = f32[262144]{0:T(1024)} async-done(((f32[262144]{0:T(1024)}), f32[262144]{0:T(1024)}) %all-reduce.4.cloned.1.call-update) | async-done | bytes 1048592 | tf_op jit(solution)/shard_map/psum | solution.py:80
  149.9 3.5 multiply_reduce_fusion.2
  153.5 1.0 reshape.95
  154.6 1.3 fusion
  155.8 4.0 fusion.20
  160.2 3.9 fusion.18
  164.2 0.8 fusion.61
  165.4 3.3 fusion.44
  169.3 1.2 copy.29
  170.6 39.6 %psum.43 = f32[]{:T(128)} all-reduce(f32[]{:T(128)} %get-tuple-element.14), channel_id=1, replica_groups=mesh['grp'=4,'dev'=8] {'grp','dev'}, use_global_device_ids=true, to_apply=%region_5.6 | all-reduce | flops 1 | bytes 8 | tf_op jit(solution)/shard_map/psum | solution.py:88
  211.7 88.9 %all-reduce.6.cloned.1.call-done = f32[262144]{0:T(1024)} async-done(((f32[262144]{0:T(1024)}), f32[262144]{0:T(1024)}) %all-reduce.6.cloned.1.call-update) | async-done | bytes 1048592 | tf_op jit(solution)/shard_map/psum | solution.py:80
  300.6 2.4 multiply_reduce_fusion.1
  303.5 3.9 fusion.16
  307.4 0.8 fusion.64
  308.4 3.3 fusion.42
  312.4 1.2 copy.30
  313.7 39.9 %psum.45 = f32[]{:T(128)} all-reduce(f32[]{:T(128)} %get-tuple-element.16), channel_id=1, replica_groups=mesh['grp'=4,'dev'=8] {'grp','dev'}, use_global_device_ids=true, to_apply=%region_9.10 | all-reduce | flops 1 | bytes 8 | tf_op jit(solution)/shard_map/psum | solution.py:88
  355.0 88.6 %all-reduce.8.cloned.1.call-done = f32[262144]{0:T(1024)} async-done(((f32[262144]{0:T(1024)}), f32[262144]{0:T(1024)}) %all-reduce.8.cloned.1.call-update) | async-done | bytes 1048592 | tf_op jit(solution)/shard_map/psum | solution.py:80
  443.6 2.1 multiply_reduce_fusion
  445.7 1.0 copy-done.3
  447.2 3.9 fusion.14
  451.1 0.9 fusion.73
  452.0 1.1 gather_fusion
  453.2 3.6 all-to-all-start
  456.7 40.5 %psum.47 = f32[]{:T(128)} all-reduce(f32[]{:T(128)} %get-tuple-element.10), channel_id=1, replica_groups=mesh['grp'=4,'dev'=8] {'grp','dev'}, use_global_device_ids=true, to_apply=%region_14.15 | all-reduce | flops 1 | bytes 8 | tf_op jit(solution)/shard_map/psum | solution.py:88
  (44 shorter events, 4.4 us)
Async XLA Ops:
  7.2 7.3 %copy-start.5 = (s32[20]{0:T(128)S(1)}, s32[20]{0:T(128)}, u32[]{:S(2)}) copy-start(s32[20]{0:T(128)} %param.10) | copy-start | bytes 244
  7.2 142.8 %copy-start.1 = (f32[262144]{0:T(1024)S(1)}, f32[262144]{0:T(1024)}, u32[]{:S(2)}) copy-start(f32[262144]{0:T(1024)} %param.16) | copy-start | bytes 3145732
  7.2 142.8 %copy-start = (f32[262144]{0:T(1024)S(1)}, f32[262144]{0:T(1024)}, u32[]{:S(2)}) copy-start(f32[262144]{0:T(1024)} %param.17) | copy-start | bytes 3145732
  7.2 142.7 %all-reduce.4.cloned.1.call-start = ((), (), s32[]{:S(2)}) async-start(), calls=%async_computation.1 | async-start | bytes 2097152 | tf_op jit(solution)/shard_map/psum | solution.py:80
  16.3 284.3 %all-reduce.6.cloned.1.call-start = ((), (), s32[]{:S(2)}) async-start(), calls=%async_computation.2 | async-start | bytes 2097152 | tf_op jit(solution)/shard_map/psum | solution.py:80
  153.5 6.3 %copy-start.4 = (bf16[262144]{0:T(1024)(128)(2,1)S(1)}, bf16[262144]{0:T(1024)(128)(2,1)}, u32[]{:S(2)}) copy-start(bf16[262144]{0:T(1024)(128)(2,1)} %get-tuple-element.9) | copy-start | bytes 1572868
  155.8 8.4 %copy-start.7 = (bf16[1024]{0:T(1024)(128)(2,1)S(1)}, bf16[1024]{0:T(1024)(128)(2,1)}, u32[]{:S(2)}) copy-start(bf16[1024]{0:T(1024)(128)(2,1)} %param.13) | copy-start | bytes 6148
  155.8 9.2 %copy-start.6 = (bf16[1024]{0:T(1024)(128)(2,1)S(1)}, bf16[1024]{0:T(1024)(128)(2,1)}, u32[]{:S(2)}) copy-start(bf16[1024]{0:T(1024)(128)(2,1)} %param.14) | copy-start | bytes 6148
  170.5 273.1 %all-reduce.8.cloned.1.call-start = ((), (), s32[]{:S(2)}) async-start(), calls=%async_computation.3 | async-start | bytes 2097152 | tf_op jit(solution)/shard_map/psum | solution.py:80
  307.4 6.1 %copy-start.8 = (s32[8]{0:T(128)S(1)}, s32[8]{0:T(128)}, u32[]{:S(2)}) copy-start(s32[8]{0:T(128)} %param.12) | copy-start | bytes 100
  307.4 136.2 %copy-start.2 = (f32[262144]{0:T(1024)S(1)}, f32[262144]{0:T(1024)}, u32[]{:S(2)}) copy-start(f32[262144]{0:T(1024)} %param.16) | copy-start | bytes 3145732
  445.7 1.0 copy-start.3
  453.2 45.4 %all-to-all-start = ((f32[8,1,128]{2,1,0:T(1,128)}), f32[8,1,128]{2,1,0:T(1,128)S(1)}, u32[]{:S(2)}, u32[]{:S(2)}) async-start(f32[8,1,128]{2,1,0:T(1,128)} %bitcast.22), calls=%async_computation | async-start | bytes 8192 | tf_op jit(solution)/shard_map/all_to_all | solution.py:92
Sparse Core Ops, SparseCore 0:
  16.4 133.4 all-reduce.3
  170.6 129.8 all-reduce.5
  313.7 129.8 all-reduce.7
where the time goes:
time: 508 us; the launch traced here: 507 us
  waiting for transfers between devices  311 us (61%)
  blocking collectives  120 us (24%)
  matrix products  33.4 us (7%)
  between operations  19.3 us (4%)
  other arithmetic  11.3 us (2%)
  local copies, waits for them, and re-layouts  8.01 us (2%)
    psum x3, waiting for transfers between devices, per_device(): gradient = lax.psum(partial_value, ('grp', 'dev'))  311 us
    psum x3, blocking collectives, per_device(): violation = lax.psum(violation_part, ('grp', 'dev'))  120 us
    dot_general x4, matrix products, row_products(): jnp.einsum('src,sc->sr', tile_set, picked, preferred_element_type=jnp.flo...  15.8 us
  transfers between devices with their start and end apart: 4, of which 3 were waited for; matrix products, arithmetic and copies ran while one was open for 0% of the time, Pallas kernels for 0%

commit v1 on v0

--- a/solution.py
+++ b/solution.py
@@ -1,6 +1,10 @@
+import functools
+
 import jax
 import jax.numpy as jnp
 from jax import lax
+from jax.experimental import pallas as pl
+from jax.experimental.pallas import tpu as pltpu
 from jax.sharding import PartitionSpec as P
 
 NCB = 256
@@ -95,6 +99,458 @@
     return (primal, dual_final, jnp.reshape(weight, (1,)))
 
 
+MESH_ID = pl.DeviceIdType.MESH
+SPLIT = 4
+
+
+def tile_split(slot_count):
+    main = slot_count // 16 * 16
+    return main, (slot_count - main) * SPLIT
+
+
+def fits(mesh_shape, slot_count, rows_per, width, blocks, column_blocks):
+    main, tail = tile_split(slot_count)
+    devices = mesh_shape["grp"] * mesh_shape["dev"]
+    rows = main + tail
+    per_group = 128
+    if main == 0 or per_group % main or rows > 96 or slot_count % 4:
+        return False
+    if tail == 0 or per_group % tail or tail % 16:
+        return False
+    if (devices * main) % 128 or (devices * tail) % 128:
+        return False
+    if rows_per != 128 or width % (128 * SPLIT) or blocks != mesh_shape["dev"]:
+        return False
+    if mesh_shape["dev"] % 2 or column_blocks > 256 or column_blocks % 16:
+        return False
+    held = slot_count * rows_per * width * 2 + 2 * devices * rows * width * 2
+    return held < 30 * 2**20
+
+
+def fused_kernel(
+    n_grp,
+    n_dev,
+    cols,
+    counts,
+    dest,
+    rows_in,
+    tiles,
+    primal_in,
+    cost_in,
+    upper_in,
+    out_primal,
+    out_dual,
+    out_weight,
+    kv,
+    pv,
+    cv,
+    uv,
+    pnow,
+    pbf,
+    hot,
+    buf,
+    stat,
+    dsend,
+    drecv,
+    local_sem,
+    piece_send,
+    piece_recv,
+    stat_send,
+    stat_recv,
+    dual_send,
+    dual_recv,
+):
+    slots, rows_per, width = tiles.shape
+    blocks = counts.shape[0]
+    n_cb = pnow.shape[0]
+    n_all = n_grp * n_dev
+    n_chip = n_dev // 2
+    main, tail = tile_split(slots)
+    rest = slots - main
+    rows = main + tail
+    sub = width // SPLIT
+    chunks = width // 128
+    g = lax.axis_index("grp")
+    d = lax.axis_index("dev")
+    core = d % 2
+    chip = d // 2
+    partner = chip * 2 + (1 - core)
+    me = g * n_dev + d
+    f32, bf16, i32 = jnp.float32, jnp.bfloat16, jnp.int32
+
+    def remote(src, dst, ssem, rsem, tg, td):
+        return pltpu.make_async_remote_copy(
+            src_ref=src,
+            dst_ref=dst,
+            send_sem=ssem,
+            recv_sem=rsem,
+            device_id={"grp": tg, "dev": td},
+            device_id_type=MESH_ID,
+        )
+
+    others = [(a, b) for a in range(n_grp) for b in range(n_dev) if a or b]
+
+    def other(a, b):
+        return (g + a) % n_grp, (d + b) % n_dev
+
+    barrier = pltpu.get_barrier_semaphore()
+    for a, b in others:
+        tg, td = other(a, b)
+        pl.semaphore_signal(
+            barrier, inc=1, device_id={"grp": tg, "dev": td}, device_id_type=MESH_ID
+        )
+    copies = [
+        pltpu.make_async_copy(primal_in, pv, local_sem.at[0]),
+        pltpu.make_async_copy(cost_in, cv, local_sem.at[1]),
+        pltpu.make_async_copy(upper_in, uv, local_sem.at[2]),
+    ]
+    part = slots // 4
+    for k in range(4):
+        copies.append(
+            pltpu.make_async_copy(
+                tiles.at[pl.ds(k * part, part)], kv.at[pl.ds(k * part, part)], local_sem.at[3 + k]
+            )
+        )
+    copies[0].start()
+    for k in range(4):
+        copies[3 + k].start()
+    copies[1].start()
+    copies[2].start()
+
+    def slot_of(pos):
+        return jnp.where(pos < main, pos, main + (pos - main) % rest)
+
+    starts = [counts[0] * 0]
+    for b in range(blocks):
+        starts.append(starts[-1] + counts[b])
+    total = starts[-1]
+    lane = lax.broadcasted_iota(i32, (1, 128), 1)
+    lane_slot = jnp.where(lane < rows, slot_of(lane), slots)
+    row = lax.broadcasted_iota(i32, (rows, 128), 0)
+    row_slot = slot_of(row)
+    row_wide = lax.broadcasted_iota(i32, (rows, n_cb), 0)
+    wide_slot = slot_of(row_wide)
+    stat_row = jnp.full((1, 128), -1.0, f32)
+    wide_col = jnp.full((rows, n_cb), -1, i32)
+    owner_of = []
+    for s in range(slots):
+        live_col = jnp.where(s < total, cols[s], -1)
+        stat_row = jnp.where(lane_slot == s, live_col.astype(f32), stat_row)
+        wide_col = jnp.where(wide_slot == s, live_col, wide_col)
+        who = jnp.int32(0)
+        for b in range(1, blocks):
+            who = who + jnp.where(starts[b] <= s, 1, 0)
+        owner_of.append(jnp.where(s < total, who, -1))
+    own_hot = jnp.where(
+        wide_col == lax.broadcasted_iota(i32, (rows, n_cb), 1), 1.0, 0.0
+    ).astype(bf16)
+    row_owner = jnp.zeros((rows, 128), i32)
+    for b in range(1, blocks):
+        row_owner = row_owner + jnp.where(row_slot >= starts[b], 1, 0)
+    row_owner = jnp.where(row_slot < total, row_owner, -1)
+    block_row = lax.broadcasted_iota(i32, (blocks, 128), 0)
+    bounds = rows_in[0]
+    dual = rows_in[1]
+
+    stat[0, me] = stat_row
+    pl.semaphore_wait(barrier, len(others))
+
+    def send_stat(turn):
+        sent = []
+        for k, (a, b) in enumerate(others):
+            tg, td = other(a, b)
+            copy = remote(
+                stat.at[turn, me],
+                stat.at[turn, me],
+                stat_send.at[turn, k],
+                stat_recv.at[turn, me],
+                tg,
+                td,
+            )
+            copy.start()
+            sent.append(copy)
+        return sent
+
+    def wait_stat(turn):
+        for a, b in others:
+            tg, td = other(a, b)
+            src = tg * n_dev + td
+            remote(
+                stat.at[turn, src],
+                stat.at[turn, src],
+                stat_send.at[turn, 0],
+                stat_recv.at[turn, src],
+                tg,
+                td,
+            ).wait_recv()
+
+    pending = send_stat(0)
+
+    def row_image_of():
+        picked = jnp.dot(own_hot, pbf[...], preferred_element_type=f32).astype(bf16)
+        chosen = jnp.zeros((rows, rows_per), f32)
+        for s in range(0, slots, 2):
+            pair = kv[s : s + 2].reshape(2 * rows_per, width)
+            both = lax.dot_general(
+                picked, pair, (((1,), (1,)), ((), ())), preferred_element_type=f32
+            )
+            chosen = jnp.where(row == s, both[:, :rows_per], chosen)
+            chosen = jnp.where(row == s + 1, both[:, rows_per:], chosen)
+        image = jnp.zeros((blocks, rows_per), f32)
+        for s in range(slots):
+            image = image + jnp.where(block_row == owner_of[s], chosen[s : s + 1, :], 0.0)
+        return image
+
+    def write_piece(p, dual_now):
+        spread = jnp.zeros((rows, rows_per), f32)
+        for b in range(blocks):
+            spread = jnp.where(row_owner == b, dual_now[b : b + 1, :], spread)
+        total_piece = jnp.zeros((rows, width), f32)
+        for s in range(0, slots, 2):
+            left = jnp.concatenate(
+                [
+                    jnp.where(row_slot == s, spread, 0.0),
+                    jnp.where(row_slot == s + 1, spread, 0.0),
+                ],
+                axis=1,
+            ).astype(bf16)
+            pair = kv[s : s + 2].reshape(2 * rows_per, width)
+            total_piece = total_piece + jnp.dot(left, pair, preferred_element_type=f32)
+        quarter = lax.broadcasted_iota(i32, (tail, sub), 0) // rest
+        ends = jnp.zeros((tail, sub), f32)
+        for q in range(SPLIT):
+            part_q = total_piece[:, q * sub : (q + 1) * sub]
+            buf[p, me, q * main : (q + 1) * main, :] = part_q[:main].astype(bf16)
+            ends = jnp.where(quarter == q, part_q[main:], ends)
+        buf[p, me, SPLIT * main : SPLIT * main + tail, :] = ends.astype(bf16)
+
+    def exchange(p, middle):
+        sent = []
+
+        def send(slot, tg, td):
+            copy = remote(
+                buf.at[p, slot],
+                buf.at[p, slot],
+                piece_send.at[len(sent)],
+                piece_recv.at[p, slot],
+                tg,
+                td,
+            )
+            copy.start()
+            sent.append(copy)
+
+        def arrived(slot):
+            remote(
+                buf.at[p, slot],
+                buf.at[p, slot],
+                piece_send.at[0],
+                piece_recv.at[p, slot],
+                g,
+                partner,
+            ).wait_recv()
+
+        def plane(slot):
+            for k in range(1, n_chip):
+                send(slot, g, ((chip + k) % n_chip) * 2 + core)
+            send(slot, g, partner)
+
+        for a in range(1, n_grp):
+            send(me, (g + a) % n_grp, d)
+        plane(me)
+        middle()
+        order = sorted(range(1, n_grp), key=lambda a: min(a, n_grp - a))
+        for a in order:
+            slot = ((g + a) % n_grp) * n_dev + d
+            arrived(slot)
+            plane(slot)
+        for a in [0] + order:
+            for k in range(1, n_chip):
+                slot = ((g + a) % n_grp) * n_dev + ((chip + k) % n_chip) * 2 + core
+                arrived(slot)
+                send(slot, g, partner)
+        for a in [0] + order:
+            for k in range(n_chip):
+                arrived(((g + a) % n_grp) * n_dev + ((chip + k) % n_chip) * 2 + (1 - core))
+        return sent
+
+    def build_hot():
+        wait_stat(0)
+        block_of = lax.broadcasted_iota(i32, (n_cb, 128), 0).astype(f32)
+        for base, size, start in ((0, main, 0), (main, tail, n_all * main)):
+            per = 128 // size
+            for group in range(n_all // per):
+                line = jnp.full((1, 128), -1.0, f32)
+                for k in range(per):
+                    shift = (k * size - base) % 128
+                    source = stat[0, group * per + k]
+                    moved = source if shift == 0 else pltpu.roll(source, shift, 1)
+                    line = jnp.where(lane // size == k, moved, line)
+                match = jnp.where(block_of == line, 1.0, 0.0)
+                if base == 0:
+                    hot[:, group * 128 : (group + 1) * 128] = match.astype(bf16)
+                else:
+                    for q in range(SPLIT):
+                        at = start + q * n_all * tail + group * 128
+                        keep = jnp.where((lane % size) // rest == q, match, 0.0)
+                        hot[:, at : at + 128] = keep.astype(bf16)
+
+    copies[0].wait()
+    for j in range(chunks):
+        value = pv[pl.ds(j, n_cb, stride=chunks), :]
+        pnow[:, j * 128 : (j + 1) * 128] = value
+        pbf[:, j * 128 : (j + 1) * 128] = value.astype(bf16)
+    for k in range(4):
+        copies[3 + k].wait()
+
+    weight = jnp.ones((1, 1), f32)
+    change = None
+    image = None
+    for it in range(ITERS):
+        p = it % 2
+        write_piece(p, dual)
+        if it == 0:
+
+            def first():
+                build_hot()
+
+            sent = exchange(p, first)
+            image = row_image_of()
+            copies[1].wait()
+            copies[2].wait()
+        else:
+            sent = exchange(p, lambda: None)
+            wait_stat(it)
+            violation = jnp.sum(stat[it], axis=0)[:, 127:128]
+            weight = jnp.sqrt(weight * jnp.sqrt((violation + 1e-06) / (change + 1e-06)))
+        tau = step_scale / weight
+        ends = buf[p, :, SPLIT * main :, :].reshape(n_all * tail, sub)
+        moved_sum = jnp.zeros((8, 128), f32)
+        for q in range(SPLIT):
+            body = buf[p, :, q * main : (q + 1) * main, :].reshape(n_all * main, sub)
+            at = n_all * main + q * n_all * tail
+            grad = jnp.dot(hot[:, : n_all * main], body, preferred_element_type=f32)
+            grad = grad + jnp.dot(
+                hot[:, at : at + n_all * tail], ends, preferred_element_type=f32
+            )
+            for h in range(sub // 128):
+                j = q * (sub // 128) + h
+                here = pl.ds(j, n_cb, stride=chunks)
+                span = slice(j * 128, (j + 1) * 128)
+                old = pnow[:, span]
+                stepped = old - tau * (cv[here, :] - grad[:, h * 128 : (h + 1) * 128])
+                new = jnp.minimum(jnp.maximum(stepped, 0.0), uv[here, :])
+                gap = new - old
+                moved_sum = moved_sum + jnp.sum((gap * gap).reshape(n_cb // 8, 8, 128), axis=0)
+                pnow[:, span] = new
+                pbf[:, span] = new.astype(bf16)
+                if it == ITERS - 1:
+                    out_primal[here, :] = new
+        change = jnp.sum(moved_sum, axis=(0, 1), keepdims=True)
+        next_image = row_image_of()
+        sigma = step_scale * weight
+        dual = jnp.maximum(dual + sigma * (bounds - (2.0 * next_image - image)), 0.0)
+        short = jnp.maximum(bounds - next_image, 0.0)
+        image = next_image
+        stat[it + 1, me] = jnp.where(
+            lane == 127, jnp.sum(short * short, axis=(0, 1), keepdims=True), 0.0
+        )
+        for copy in pending:
+            copy.wait_send()
+        for copy in sent:
+            copy.wait_send()
+        pending = send_stat(it + 1)
+
+    for e in range(n_dev):
+        line = jnp.zeros((1, rows_per), f32)
+        for k in range(blocks):
+            line = jnp.where(dest[k] == e, dual[k : k + 1, :], line)
+        dsend[e] = line
+    sent = []
+    for k in range(1, n_dev):
+        td = (d + k) % n_dev
+        copy = remote(dsend.at[td], drecv.at[d], dual_send.at[k], dual_recv.at[d], g, td)
+        copy.start()
+        sent.append(copy)
+    drecv[d] = dsend[d]
+    wait_stat(ITERS)
+    violation = jnp.sum(stat[ITERS], axis=0)[:, 127:128]
+    weight = jnp.sqrt(weight * jnp.sqrt((violation + 1e-06) / (change + 1e-06)))
+    out_weight[...] = jnp.broadcast_to(weight, (1, 128))
+    for k in range(1, n_dev):
+        src = (d + k) % n_dev
+        remote(dsend.at[src], drecv.at[src], dual_send.at[k], dual_recv.at[src], g, src).wait_recv()
+    out_dual[...] = drecv[...]
+    for copy in pending:
+        copy.wait_send()
+    for copy in sent:
+        copy.wait_send()
+
+
+def fused_device(mesh_shape, *args):
+    tiles, cols, counts, dest, row_bounds, dual_start, primal, cost, upper = args
+    slots, rows_per, width = tiles.shape
+    blocks = counts.shape[0]
+    column_blocks = primal.shape[0] // width
+    if not fits(mesh_shape, slots, rows_per, width, blocks, column_blocks):
+        return per_device(*args)
+    n_grp, n_dev = mesh_shape["grp"], mesh_shape["dev"]
+    n_all = n_grp * n_dev
+    main, tail = tile_split(slots)
+    rows_in = (
+        jnp.stack([row_bounds, dual_start]).astype(jnp.float32).reshape(2, blocks, rows_per)
+    )
+    flat = (primal.shape[0] // 128, 128)
+    f32, bf16 = jnp.float32, jnp.bfloat16
+    vmem = pl.BlockSpec(memory_space=pltpu.VMEM)
+    smem = pl.BlockSpec(memory_space=pltpu.SMEM)
+    anywhere = pl.BlockSpec(memory_space=pl.ANY)
+    sends = (n_grp - 1) + n_grp * (n_dev // 2) + n_grp * (n_dev // 2 - 1)
+    out_primal, out_dual, out_weight = pl.pallas_call(
+        functools.partial(fused_kernel, n_grp, n_dev),
+        name="pdhg_fused",
+        out_shape=(
+            jax.ShapeDtypeStruct(flat, f32),
+            jax.ShapeDtypeStruct((n_dev, 1, rows_per), f32),
+            jax.ShapeDtypeStruct((1, 128), f32),
+        ),
+        in_specs=[smem, smem, smem, vmem, anywhere, anywhere, anywhere, anywhere],
+        out_specs=(vmem, vmem, vmem),
+        scratch_shapes=[
+            pltpu.VMEM((slots, rows_per, width), bf16),
+            pltpu.VMEM(flat, f32),
+            pltpu.VMEM(flat, f32),
+            pltpu.VMEM(flat, f32),
+            pltpu.VMEM((column_blocks, width), f32),
+            pltpu.VMEM((column_blocks, width), bf16),
+            pltpu.VMEM((column_blocks, n_all * (main + SPLIT * tail)), bf16),
+            pltpu.VMEM((2, n_all, SPLIT * main + tail, width // SPLIT), bf16),
+            pltpu.VMEM((ITERS + 1, n_all, 1, 128), f32),
+            pltpu.VMEM((n_dev, 1, rows_per), f32),
+            pltpu.VMEM((n_dev, 1, rows_per), f32),
+            pltpu.SemaphoreType.DMA((7,)),
+            pltpu.SemaphoreType.DMA((sends,)),
+            pltpu.SemaphoreType.DMA((2, n_all)),
+            pltpu.SemaphoreType.DMA((ITERS + 1, n_all)),
+            pltpu.SemaphoreType.DMA((ITERS + 1, n_all)),
+            pltpu.SemaphoreType.DMA((n_dev,)),
+            pltpu.SemaphoreType.DMA((n_dev,)),
+        ],
+        compiler_params=pltpu.CompilerParams(
+            collective_id=0, has_side_effects=True, vmem_limit_bytes=48 * 2**20
+        ),
+    )(
+        cols,
+        counts,
+        dest,
+        rows_in,
+        tiles,
+        primal.reshape(flat),
+        cost.reshape(flat),
+        upper.reshape(flat),
+    )
+    return out_primal.reshape(-1), out_dual.reshape(-1), out_weight[0, :1]
+
+
 def solution(mesh):
     in_specs = (
         P(("grp", "dev"), None, None),
@@ -109,5 +565,9 @@
     )
     out_specs = (P(), P(("grp", "dev")), P())
     return jax.shard_map(
-        per_device, mesh=mesh, in_specs=in_specs, out_specs=out_specs, check_vma=False
-    )
+        functools.partial(fused_device, dict(mesh.shape)),
+        mesh=mesh,
+        in_specs=in_specs,
+        out_specs=out_specs,
+        check_vma=False,
+    )

time: 508 us -> 78.1 us (0.15)
  waiting for transfers between devices: 311 us -> 0 us
  blocking collectives: 120 us -> 0 us
  Pallas kernels: 0 us -> 68 us
  matrix products: 33.4 us -> 0 us
  between operations: 19.3 us -> 1.81 us
  other arithmetic: 11.3 us -> 0.7 us
    psum x3 -> x0, waiting for transfers between devices: 311 us -> none  [per_device(): gradient = lax.psum(partial_value, ('grp', 'dev'))]
    psum x3 -> x0, blocking collectives: 120 us -> none  [per_device(): violation = lax.psum(violation_part, ('grp', 'dev'))]
    pallas_call x0 -> x1, Pallas kernels: none -> 68 us  [fused_device(): pl.pallas_call(functools.partial(fused_kernel, n_grp, n_dev), name='pdhg_...]
    dot_general x21 -> x0, matrix products: 33.4 us -> none  [the longest x4 15.8 us: row_products(): jnp.einsum('src,sc->sr', tile_set, picked, preferred_element_type=jnp.flo...]
    reduce_sum x6 -> x0, other arithmetic: 9.55 us -> none  [the longest x3 8.06 us: per_device(): change = jnp.sum((primal_next - primal) ** 2)]
  transfers between devices with their start and end apart: 4 -> 0, of which waited for: 3 -> 0; matrix products, arithmetic and copies ran while one was open for 0% -> 0% of each run, Pallas kernels for 0% -> 0%
where the time goes in v1:
time: 78.1 us; the launch traced here: 77.8 us
  Pallas kernels  68 us (87%)
  local copies, waits for them, and re-layouts  7.27 us (9%)
  between operations  1.81 us (2%)
    pallas_call x1, Pallas kernels, fused_device(): pl.pallas_call(functools.partial(fused_kernel, n_grp, n_dev), name='pdhg_...  68 us
    unnamed x14, local copies, waits for them, and re-layouts  7.27 us

profile of v1, /device:TPU:0, one launch (start us, length us, event | category | flops | bytes accessed | tf_op | source)
XLA Modules:
  0.0 77.8 jit_solution(12242588670870883583)
XLA Ops:
  0.6 0.7 maximum_convert_fusion.rows_in
  1.3 0.0 copy-start
  1.3 1.2 %copy-done = f32[262144]{0:T(1024)S(1)} copy-done((f32[262144]{0:T(1024)S(1)}, f32[262144]{0:T(1024)}, u32[]{:S(2)}) %copy-start) | copy-done | bytes 1048600
  2.6 0.0 copy-start.1
  2.6 1.2 %copy-done.1 = f32[262144]{0:T(1024)S(1)} copy-done((f32[262144]{0:T(1024)S(1)}, f32[262144]{0:T(1024)}, u32[]{:S(2)}) %copy-start.1) | copy-done | bytes 1048600
  3.8 0.0 copy-start.2
  3.8 1.2 %copy-done.2 = f32[262144]{0:T(1024)S(1)} copy-done((f32[262144]{0:T(1024)S(1)}, f32[262144]{0:T(1024)}, u32[]{:S(2)}) %copy-start.2) | copy-done | bytes 1048600
  5.0 0.0 copy-start.3
  5.0 0.7 copy-done.3
  5.7 0.0 copy-start.4
  5.7 0.7 copy-done.4
  6.3 0.0 copy-start.5
  6.3 0.7 copy-done.5
  7.0 68.0 %pdhg_fused.1 = (f32[2048,128]{1,0:T(8,128)S(1)}, f32[8,1,128]{2,1,0:T(1,128)S(1)}, f32[1,128]{1,0:T(1,128)S(1)}) custom-call(s32[20]{0:T(128)S(1)} %copy-done.3, s32[8]{0:T(128)S(1)} %copy-done.4, s32[8]{0:T(128)S(1)} %copy-done.5, f32[2,8,128]{2,1,0:T(8,128)S(1)} %maximum_convert_fusion.rows_in, bf16[20,128,1024]{2,1,0:T(8,128)(2,1)} %tiles.1, ...), custom_call_target="tpu_custom_call" | custom-call | tf_op jit(solution)/shard_map/pdhg_fused/pallas_call | solution.py:508
  75.0 1.0 %copy.15 = f32[262144]{0:T(1024)} copy(f32[262144]{0:T(1024)S(1)} %bitcast.9) | data formatting | bytes 2097152
  76.0 0.6 copy.16
Async XLA Ops:
  1.3 1.2 %copy-start = (f32[262144]{0:T(1024)S(1)}, f32[262144]{0:T(1024)}, u32[]{:S(2)}) copy-start(f32[262144]{0:T(1024)} %param.15) | copy-start | bytes 3145732
  2.6 1.2 %copy-start.1 = (f32[262144]{0:T(1024)S(1)}, f32[262144]{0:T(1024)}, u32[]{:S(2)}) copy-start(f32[262144]{0:T(1024)} %param.16) | copy-start | bytes 3145732
  3.8 1.2 %copy-start.2 = (f32[262144]{0:T(1024)S(1)}, f32[262144]{0:T(1024)}, u32[]{:S(2)}) copy-start(f32[262144]{0:T(1024)} %param.17) | copy-start | bytes 3145732
  5.0 0.7 copy-start.3
  5.7 0.7 copy-start.4
  6.3 0.7 copy-start.5

commit v2 on v1

--- a/solution.py
+++ b/solution.py
@@ -130,9 +130,7 @@
 def fused_kernel(
     n_grp,
     n_dev,
-    cols,
-    counts,
-    dest,
+    indices,
     rows_in,
     tiles,
     primal_in,
@@ -161,7 +159,10 @@
     dual_recv,
 ):
     slots, rows_per, width = tiles.shape
-    blocks = counts.shape[0]
+    blocks = rows_in.shape[1]
+    cols = [indices[k] for k in range(slots)]
+    counts = [indices[slots + k] for k in range(blocks)]
+    dest = [indices[slots + blocks + k] for k in range(blocks)]
     n_cb = pnow.shape[0]
     n_all = n_grp * n_dev
     n_chip = n_dev // 2
@@ -204,16 +205,17 @@
         pltpu.make_async_copy(cost_in, cv, local_sem.at[1]),
         pltpu.make_async_copy(upper_in, uv, local_sem.at[2]),
     ]
-    part = slots // 4
-    for k in range(4):
+    part = 4
+    parts = slots // part
+    for k in range(parts):
         copies.append(
             pltpu.make_async_copy(
                 tiles.at[pl.ds(k * part, part)], kv.at[pl.ds(k * part, part)], local_sem.at[3 + k]
             )
         )
+    for k in range(parts):
+        copies[3 + k].start()
     copies[0].start()
-    for k in range(4):
-        copies[3 + k].start()
     copies[1].start()
     copies[2].start()
 
@@ -301,12 +303,14 @@
             image = image + jnp.where(block_row == owner_of[s], chosen[s : s + 1, :], 0.0)
         return image
 
-    def write_piece(p, dual_now):
+    def write_piece(p, dual_now, loading):
         spread = jnp.zeros((rows, rows_per), f32)
         for b in range(blocks):
             spread = jnp.where(row_owner == b, dual_now[b : b + 1, :], spread)
         total_piece = jnp.zeros((rows, width), f32)
         for s in range(0, slots, 2):
+            if loading and s % part == 0:
+                copies[3 + s // part].wait()
             left = jnp.concatenate(
                 [
                     jnp.where(row_slot == s, spread, 0.0),
@@ -324,7 +328,7 @@
             ends = jnp.where(quarter == q, part_q[main:], ends)
         buf[p, me, SPLIT * main : SPLIT * main + tail, :] = ends.astype(bf16)
 
-    def exchange(p, middle):
+    def exchange(p, middle, later):
         sent = []
 
         def send(slot, tg, td):
@@ -363,6 +367,7 @@
             slot = ((g + a) % n_grp) * n_dev + d
             arrived(slot)
             plane(slot)
+        later()
         for a in [0] + order:
             for k in range(1, n_chip):
                 slot = ((g + a) % n_grp) * n_dev + ((chip + k) % n_chip) * 2 + core
@@ -394,31 +399,33 @@
                         keep = jnp.where((lane % size) // rest == q, match, 0.0)
                         hot[:, at : at + 128] = keep.astype(bf16)
 
-    copies[0].wait()
-    for j in range(chunks):
-        value = pv[pl.ds(j, n_cb, stride=chunks), :]
-        pnow[:, j * 128 : (j + 1) * 128] = value
-        pbf[:, j * 128 : (j + 1) * 128] = value.astype(bf16)
-    for k in range(4):
-        copies[3 + k].wait()
-
     weight = jnp.ones((1, 1), f32)
     change = None
     image = None
     for it in range(ITERS):
         p = it % 2
-        write_piece(p, dual)
+        write_piece(p, dual, it == 0)
         if it == 0:
 
+            images = []
+
             def first():
+                copies[0].wait()
+                for j in range(chunks):
+                    value = pv[pl.ds(j, n_cb, stride=chunks), :]
+                    pnow[:, j * 128 : (j + 1) * 128] = value
+                    pbf[:, j * 128 : (j + 1) * 128] = value.astype(bf16)
                 build_hot()
 
-            sent = exchange(p, first)
-            image = row_image_of()
-            copies[1].wait()
-            copies[2].wait()
+            def second():
+                images.append(row_image_of())
+                copies[1].wait()
+                copies[2].wait()
+
+            sent = exchange(p, first, second)
+            image = images[0]
         else:
-            sent = exchange(p, lambda: None)
+            sent = exchange(p, lambda: None, lambda: None)
             wait_stat(it)
             violation = jnp.sum(stat[it], axis=0)[:, 127:128]
             weight = jnp.sqrt(weight * jnp.sqrt((violation + 1e-06) / (change + 1e-06)))
@@ -444,7 +451,10 @@
                 pnow[:, span] = new
                 pbf[:, span] = new.astype(bf16)
                 if it == ITERS - 1:
-                    out_primal[here, :] = new
+                    pv[here, :] = new
+        if it == ITERS - 1:
+            leaving = pltpu.make_async_copy(pv, out_primal, local_sem.at[0])
+            leaving.start()
         change = jnp.sum(moved_sum, axis=(0, 1), keepdims=True)
         next_image = row_image_of()
         sigma = step_scale * weight
@@ -480,6 +490,7 @@
         src = (d + k) % n_dev
         remote(dsend.at[src], drecv.at[src], dual_send.at[k], dual_recv.at[src], g, src).wait_recv()
     out_dual[...] = drecv[...]
+    leaving.wait()
     for copy in pending:
         copy.wait_send()
     for copy in sent:
@@ -503,7 +514,7 @@
     f32, bf16 = jnp.float32, jnp.bfloat16
     vmem = pl.BlockSpec(memory_space=pltpu.VMEM)
     smem = pl.BlockSpec(memory_space=pltpu.SMEM)
-    anywhere = pl.BlockSpec(memory_space=pl.ANY)
+    far = pl.BlockSpec(memory_space=pltpu.HBM)
     sends = (n_grp - 1) + n_grp * (n_dev // 2) + n_grp * (n_dev // 2 - 1)
     out_primal, out_dual, out_weight = pl.pallas_call(
         functools.partial(fused_kernel, n_grp, n_dev),
@@ -513,8 +524,8 @@
             jax.ShapeDtypeStruct((n_dev, 1, rows_per), f32),
             jax.ShapeDtypeStruct((1, 128), f32),
         ),
-        in_specs=[smem, smem, smem, vmem, anywhere, anywhere, anywhere, anywhere],
-        out_specs=(vmem, vmem, vmem),
+        in_specs=[smem, vmem, far, far, far, far],
+        out_specs=(far, vmem, vmem),
         scratch_shapes=[
             pltpu.VMEM((slots, rows_per, width), bf16),
             pltpu.VMEM(flat, f32),
@@ -527,7 +538,7 @@
             pltpu.VMEM((ITERS + 1, n_all, 1, 128), f32),
             pltpu.VMEM((n_dev, 1, rows_per), f32),
             pltpu.VMEM((n_dev, 1, rows_per), f32),
-            pltpu.SemaphoreType.DMA((7,)),
+            pltpu.SemaphoreType.DMA((3 + slots // 4,)),
             pltpu.SemaphoreType.DMA((sends,)),
             pltpu.SemaphoreType.DMA((2, n_all)),
             pltpu.SemaphoreType.DMA((ITERS + 1, n_all)),
@@ -536,12 +547,10 @@
             pltpu.SemaphoreType.DMA((n_dev,)),
         ],
         compiler_params=pltpu.CompilerParams(
-            collective_id=0, has_side_effects=True, vmem_limit_bytes=48 * 2**20
+            collective_id=0, has_side_effects=True, vmem_limit_bytes=65 * 10**6
         ),
     )(
-        cols,
-        counts,
-        dest,
+        jnp.concatenate([cols, counts, dest]),
         rows_in,
         tiles,
         primal.reshape(flat),

time: 78.1 us -> 75.9 us (0.972)
  local copies, waits for them, and re-layouts: 7.27 us -> 3.53 us
  other arithmetic: 0.7 us -> 2.57 us
  Pallas kernels: 68 us -> 67.1 us
    unnamed x14 -> x2, local copies, waits for them, and re-layouts: 7.27 us -> 3.53 us
    concatenate x0 -> x1, other arithmetic: none -> 1.27 us  [fused_device(): jnp.concatenate([cols, counts, dest])]
    pallas_call x1, Pallas kernels: 68 us -> 67.1 us  [fused_device(): pl.pallas_call(functools.partial(fused_kernel, n_grp, n_dev), name='pdhg_...]
where the time goes in v2:
time: 75.9 us; the launch traced here: 75.6 us
  Pallas kernels  67.1 us (88%)
  local copies, waits for them, and re-layouts  3.53 us (5%)
  other arithmetic  2.57 us (3%)
  between operations  2.4 us (3%)
    pallas_call x1, Pallas kernels, fused_device(): pl.pallas_call(functools.partial(fused_kernel, n_grp, n_dev), name='pdhg_...  67.1 us
    unnamed x2, local copies, waits for them, and re-layouts  3.53 us

profile of v2, /device:TPU:0, one launch (start us, length us, event | category | flops | bytes accessed | tf_op | source)
XLA Modules:
  0.0 75.6 jit_solution(4752829533367166003)
XLA Ops:
  0.6 1.3 %pad_add_fusion.indices = s32[36]{0:T(128)} fusion(s32[8]{0:T(128)} %param.12, s32[8]{0:T(128)} %param.11, s32[20]{0:T(128)} %param.10), kind=kLoop, calls=%fused_computation.1 | loop fusion | flops 72 | bytes 288 | tf_op jit(solution)/shard_map/concatenate | solution.py:553
  1.9 1.3 %maximum_convert_fusion.rows_in = f32[2,8,128]{2,1,0:T(8,128)} fusion(bf16[1,8,128]{2,1,0:T(8,128)(2,1)} %bitcast.14, bf16[1,8,128]{2,1,0:T(8,128)(2,1)} %bitcast.15), kind=kLoop, calls=%fused_computation | loop fusion | flops 4096 | bytes 12288 | tf_op jit(solution)/shard_map/convert_element_type | solution.py:511
  3.2 67.1 %pdhg_fused.1 = (f32[2048,128]{1,0:T(8,128)}, f32[8,1,128]{2,1,0:T(1,128)}, f32[1,128]{1,0:T(1,128)}) custom-call(s32[36]{0:T(128)} %pad_add_fusion.indices, f32[2,8,128]{2,1,0:T(8,128)} %maximum_convert_fusion.rows_in, bf16[20,128,1024]{2,1,0:T(8,128)(2,1)} %tiles.1, f32[2048,128]{1,0:T(8,128)} %bitcast.9, f32[2048,128]{1,0:T(8,128)} %bitcast.10, ...), custom_call_target="tpu_custom_call" | custom-call | tf_op jit(solution)/shard_map/pdhg_fused/pallas_call | solution.py:519
  70.3 2.3 %copy.15 = f32[262144]{0:T(1024)} copy(f32[262144]{0:T(1024)} %bitcast.12) | data formatting | bytes 2097152
  72.6 1.3 %copy.16 = f32[1024]{0:T(1024)} copy(f32[1024]{0:T(1024)} %bitcast.13) | data formatting | bytes 8192
